TPU v7x, 32 devices: a whole 2x2x4 slice. The times are simulated.
32 devices in a mesh: dp: 2 (over x), expert: 4 (over y, core), sample: 4 (over z).
Axes of the slice: x: 2, y: 2, z: 4, core: 2. Of those that a mesh axis runs over, the one named last changes fastest.
Arguments:
- tokens: bfloat16 [640, 4096], P(('dp', 'expert', 'sample')), may hold values from -6 to 6
- cotangent: bfloat16 [640, 4096], P(('dp', 'expert', 'sample')), may hold values from -6 to 6
- routes: int32 [640, 2], P(('dp', 'expert', 'sample')), may hold values from 0 to 7, all different within a row; in each aligned block of 20 rows (0 to 19, 20 to 39, ...) at most 6 rows name the same one
- gate_weights: float32 [640, 2], P(('dp', 'expert', 'sample')), may hold values from 0.1 to 1
- lengths: int32 [8, 4], P(('dp', 'expert'), 'sample'), may hold values from 1 to 20
- rewards: int32 [8, 4], P(('dp', 'expert'), 'sample'), may hold values from -48 to 48
- w_gate: bfloat16 [8, 8192, 4096], P('expert', ('dp', 'sample')), may hold values from -0.09375 to 0.09375
- w_up: bfloat16 [8, 8192, 4096], P('expert', ('dp', 'sample')), may hold values from -0.09375 to 0.09375
- w_down: bfloat16 [8, 8192, 4096], P('expert', ('dp', 'sample')), may hold values from -0.0625 to 0.0625
Outputs:
- grad_tokens: bfloat16 [640, 4096], P(('dp', 'expert', 'sample'))
- grad_w_gate: bfloat16 [8, 8192, 4096], P('expert', ('dp', 'sample'))
- grad_w_up: bfloat16 [8, 8192, 4096], P('expert', ('dp', 'sample'))
- grad_w_down: bfloat16 [8, 8192, 4096], P('expert', ('dp', 'sample'))
Inputs may be any that keep to these rules, and one draw needn't show every extreme that they name: `routes`: each row names 2 different experts; among the rows of one device no expert is named by more than 6 rows, and in every draw some device's rows name some expert exactly 6 times.
All inputs are finite; a program needn't handle non-finite values.
Results may differ from a plain program's by a relative error of at most 0.025.
Values may be sent and summed in bfloat16 or wider, within the bound.
A program may use at most 192 MiB of HBM per device.

v0:
```python
import jax
import jax.numpy as jnp
from jax import lax
from jax.sharding import PartitionSpec as P

CAP = 6


def silu_parts(pre_gate):
    gate_prob = jax.nn.sigmoid(pre_gate)
    return (pre_gate * gate_prob, gate_prob * (1.0 + pre_gate * (1.0 - gate_prob)))


def expert_rows(inputs, grads_out, w_gate, w_up, w_down):
    pre_gate = jnp.einsum("rjcd,jfd->rjcf", inputs, w_gate, preferred_element_type=jnp.float32)
    pre_up = jnp.einsum("rjcd,jfd->rjcf", inputs, w_up, preferred_element_type=jnp.float32)
    active, derivative = silu_parts(pre_gate)
    hidden = (active * pre_up).astype(jnp.bfloat16)
    grad_hidden = jnp.einsum(
        "rjcd,jfd->rjcf", grads_out, w_down, preferred_element_type=jnp.float32
    )
    grad_gate = (grad_hidden * pre_up * derivative).astype(jnp.bfloat16)
    grad_up = (grad_hidden * active).astype(jnp.bfloat16)
    return (hidden, grad_gate, grad_up)


def weight_terms(inputs, grads_out, hidden, grad_gate, grad_up):
    term_gate = jnp.einsum("rjcf,rjcd->jfd", grad_gate, inputs, preferred_element_type=jnp.float32)
    term_up = jnp.einsum("rjcf,rjcd->jfd", grad_up, inputs, preferred_element_type=jnp.float32)
    term_down = jnp.einsum("rjcf,rjcd->jfd", hidden, grads_out, preferred_element_type=jnp.float32)
    return (term_gate, term_up, term_down)


def input_terms(grad_gate, grad_up, w_gate, w_up):
    from_gate = jnp.einsum("rjcf,jfd->rjcd", grad_gate, w_gate, preferred_element_type=jnp.float32)
    from_up = jnp.einsum("rjcf,jfd->rjcd", grad_up, w_up, preferred_element_type=jnp.float32)
    return from_gate + from_up


def send_sum(blocks, axis):
    count = lax.axis_size(axis)
    me = lax.axis_index(axis)
    total = lax.dynamic_index_in_dim(blocks, me, 0, keepdims=False).astype(jnp.float32)
    for step in range(1, count):
        outgoing = lax.dynamic_index_in_dim(blocks, (me + step) % count, 0, keepdims=False)
        perm = [(i, (i + step) % count) for i in range(count)]
        total = total + lax.ppermute(outgoing, axis, perm).astype(jnp.float32)
    return total.astype(jnp.bfloat16)


def local(tokens, cotangent, routes, gate_weights, lengths, rewards, w_gate, w_up, w_down):
    samples = lax.axis_size("sample")
    own_reward = rewards.astype(jnp.float32) * 0.0625
    reward_total = own_reward
    for step in range(1, samples):
        perm = [(i, (i + step) % samples) for i in range(samples)]
        reward_total = reward_total + lax.ppermute(own_reward, "sample", perm)
    advantage = own_reward - (reward_total - own_reward) / (samples - 1)
    token_count = tokens.shape[0]
    model_width = tokens.shape[1]
    choices_per = routes.shape[1]
    local_experts = w_gate.shape[0]
    expert_groups = lax.axis_size("expert")
    all_experts = local_experts * expert_groups
    positions = jnp.arange(token_count, dtype=jnp.int32)
    weight_row = jnp.where(positions < lengths[0, 0], -advantage[0, 0], jnp.zeros((), jnp.float32))
    pair_scale = (gate_weights * weight_row[:, None]).reshape(-1)
    pair_expert = routes.reshape(-1)
    member = (pair_expert[:, None] == jnp.arange(all_experts, dtype=jnp.int32)[None, :]).astype(
        jnp.int32
    )
    earlier = jnp.sum((jnp.cumsum(member, axis=0) - member) * member, axis=1)
    target = pair_expert * CAP + earlier
    slot_ids = jnp.arange(all_experts * CAP, dtype=jnp.int32)
    placed = target[:, None] == slot_ids[None, :]
    chosen = jnp.sum(
        placed.reshape(token_count, choices_per, -1).astype(jnp.float32), axis=1
    ).astype(jnp.bfloat16)
    slot_scale = jnp.sum(jnp.where(placed, pair_scale[:, None], jnp.zeros((), jnp.float32)), axis=0)
    sent_inputs = jnp.dot(chosen.T, tokens, preferred_element_type=jnp.float32).astype(jnp.bfloat16)
    sent_cotangent = jnp.dot(chosen.T, cotangent, preferred_element_type=jnp.float32)
    sent_grads = (sent_cotangent * slot_scale[:, None]).astype(jnp.bfloat16)
    layout = (expert_groups, local_experts, CAP, model_width)
    arrived_inputs, arrived_grads = (
        lax.all_to_all(
            sent_inputs.reshape(layout), "expert", split_axis=0, concat_axis=0, tiled=True
        ),
        lax.all_to_all(
            sent_grads.reshape(layout), "expert", split_axis=0, concat_axis=0, tiled=True
        ),
    )
    group_inputs, group_grads = (
        lax.all_gather(arrived_inputs, ("dp", "sample"), axis=0, tiled=True),
        lax.all_gather(arrived_grads, ("dp", "sample"), axis=0, tiled=True),
    )
    hidden, grad_gate, grad_up = expert_rows(group_inputs, group_grads, w_gate, w_up, w_down)
    term_gate, term_up, term_down = weight_terms(
        group_inputs, group_grads, hidden, grad_gate, grad_up
    )
    parts = input_terms(grad_gate, grad_up, w_gate, w_up).astype(jnp.bfloat16)
    dp_size = lax.axis_size("dp")
    parts = parts.reshape(dp_size, samples, all_experts * CAP, model_width)
    row_sums = send_sum(send_sum(parts, "dp"), "sample").reshape(layout)
    returned = lax.all_to_all(row_sums, "expert", split_axis=0, concat_axis=0, tiled=True)
    flat_back = returned.reshape(all_experts * CAP, model_width)
    grad_tokens = jnp.dot(chosen, flat_back, preferred_element_type=jnp.float32).astype(
        jnp.bfloat16
    )
    return (
        grad_tokens,
        term_gate.astype(jnp.bfloat16),
        term_up.astype(jnp.bfloat16),
        term_down.astype(jnp.bfloat16),
    )


def solution(mesh):
    in_specs = (
        P(("dp", "expert", "sample"), None),
        P(("dp", "expert", "sample"), None),
        P(("dp", "expert", "sample"), None),
        P(("dp", "expert", "sample"), None),
        P(("dp", "expert"), "sample"),
        P(("dp", "expert"), "sample"),
        P("expert", ("dp", "sample"), None),
        P("expert", ("dp", "sample"), None),
        P("expert", ("dp", "sample"), None),
    )
    out_specs = (
        P(("dp", "expert", "sample"), None),
        P("expert", ("dp", "sample"), None),
        P("expert", ("dp", "sample"), None),
        P("expert", ("dp", "sample"), None),
    )
    return jax.shard_map(local, mesh=mesh, in_specs=in_specs, out_specs=out_specs, check_vma=False)
```

profile of v0, /device:TPU:0, one launch (start us, length us, event | category | flops | bytes accessed | tf_op | source)
XLA Modules:
  0.0 286.8 jit_solution(2419793541942767327)
XLA Ops:
  7.2 0.0 copy-start
  7.2 0.0 all-gather.5.cloned.1.call-start
  7.2 0.9 copy.71
  8.1 0.1 eq.40
  8.2 0.1 fusion.37
  8.3 0.1 reduce_window_sum.11
  8.4 0.2 select_reduce_fusion.1
  8.6 0.1 reduce_sum.30
  8.7 0.1 copy.72
  8.8 0.7 multiply_add_fusion
  9.4 0.1 copy.73
  9.5 0.1 fusion.36
  9.7 0.0 copy-start.7
  9.7 0.3 convolution_convert_fusion
  10.0 0.1 reshape.56
  10.1 0.4 copy.77
  10.5 11.6 %all_to_all.15 = bf16[4,2,6,4096]{3,1,2,0:T(2,128)(2,1)} all-to-all(bf16[4,2,6,4096]{3,1,2,0:T(2,128)(2,1)S(1)} %copy.77), channel_id=1, replica_groups=mesh['dp'=2,'expert'=4,'sample'=4] {'expert'}, dimensions={0} | all-to-all | bytes 786432 | tf_op jit(solution)/shard_map/all_to_all | solution.py:85
  22.1 0.0 all-gather.5.cloned.1.call-update
  22.1 0.0 all-gather.3.cloned.1.call-start
  22.8 5.3 %collective-permute-start.2 = (f32[1,1]{1,0:T(1,128)}, f32[1,1]{1,0:T(1,128)}, u32[]{:S(2)}, u32[]{:S(2)}) collective-permute-start(f32[1,1]{1,0:T(1,128)} %mul.63), channel_id=1, source_target_pairs={{0,3},{1,0},{2,1},{3,2},{4,7},{5,4},{6,5},{7,6},{8,11},{9,8},{10,9... | collective-permute-start | bytes 20 | tf_op jit(solution)/shard_map/ppermute | solution.py:57
  28.2 1.3 collective-permute-start.1
  29.5 2.3 collective-permute-start
  32.4 2.5 collective-permute-done
  36.9 0.1 copy.74
  37.0 0.1 broadcast_in_dim.29
  37.1 0.1 select_reduce_fusion
  37.2 0.3 fusion.15
  37.5 0.1 reshape.55
  37.6 0.4 copy.75
  38.0 10.5 %all_to_all.16 = bf16[4,2,6,4096]{3,1,2,0:T(2,128)(2,1)} all-to-all(bf16[4,2,6,4096]{3,1,2,0:T(2,128)(2,1)S(1)} %copy.75), channel_id=1, replica_groups=mesh['dp'=2,'expert'=4,'sample'=4] {'expert'}, dimensions={0} | all-to-all | bytes 786432 | tf_op jit(solution)/shard_map/all_to_all | solution.py:88
  48.5 0.0 all-gather.3.cloned.1.call-update
  48.6 34.4 %all-gather.5.cloned.1.call-done = bf16[32,2,6,4096]{3,1,2,0:T(2,128)(2,1)} async-done(((bf16[4,2,6,4096]{3,1,2,0:T(2,128)(2,1)}), bf16[32,2,6,4096]{3,1,2,0:T(2,128)(2,1)}) %all-gather.5.cloned.1.call-update) | async-done | bytes 3145744 | tf_op jit(solution)/shard_map/all_gather | solution.py:93
  83.0 15.3 %fusion.2 = f32[2,32,6,1024]{3,1,2,0:T(8,128)} fusion(bf16[2,1024,4096]{2,1,0:T(8,128)(2,1)} %param.15, bf16[32,2,6,4096]{3,1,2,0:T(2,128)(2,1)} %all-gather.5.cloned.1.call-done), kind=kOutput, calls=%fused_computation.5 | convolution fusion | flops 3221225472 | bytes 21495808 | tf_op jit(solution)/shard_map/rjcd,jfd->rjcf/dot_general | solution.py:15
  98.3 14.6 %fusion.8 = f32[2,32,6,1024]{3,1,2,0:T(8,128)} fusion(bf16[2,1024,4096]{2,1,0:T(8,128)(2,1)} %param.16, bf16[32,2,6,4096]{3,1,2,0:T(2,128)(2,1)S(1)} %copy-done.10), kind=kOutput, calls=%fused_computation.11 | convolution fusion | flops 3221225472 | bytes 21495808 | tf_op jit(solution)/shard_map/rjcd,jfd->rjcf/dot_general | solution.py:16
  112.8 31.0 %all-gather.3.cloned.1.call-done = bf16[32,2,6,4096]{3,1,2,0:T(2,128)(2,1)} async-done(((bf16[4,2,6,4096]{3,1,2,0:T(2,128)(2,1)}), bf16[32,2,6,4096]{3,1,2,0:T(2,128)(2,1)}) %all-gather.3.cloned.1.call-update) | async-done | bytes 3145744 | tf_op jit(solution)/shard_map/all_gather | solution.py:94
  143.8 15.0 %fusion.31 = (bf16[32,2,6,1024]{3,0,2,1:T(8,128)(2,1)S(1)}, bf16[32,2,6,1024]{3,0,2,1:T(8,128)(2,1)S(1)}) fusion(f32[2,32,6,1024]{3,1,2,0:T(8,128)} %fusion.2, f32[2,32,6,1024]{3,1,2,0:T(8,128)} %fusion.8, bf16[2,1024,4096]{2,1,0:T(8,128)(2,1)} %param.17, bf16[32,2,6,4096]{3,1,2,0:T(2,128)(2,1)} %all-gather.3.cloned.1.call-done), kind=kOutput, calls=%fused_computation.41 | convolution fusion | flops 3226337280 | bytes 24641536 | tf_op jit(solution)/shard_map/rjcd,jfd->rjcf/dot_general | solution.py:19
  158.8 8.4 %fusion = f32[2,32,6,4096]{3,1,2,0:T(8,128)S(1)} fusion(bf16[32,2,6,1024]{3,0,2,1:T(8,128)(2,1)S(1)} %get-tuple-element.5, bf16[2,1024,4096]{2,1,0:T(8,128)(2,1)} %param.15), kind=kOutput, calls=%fused_computation.3 | convolution fusion | flops 3221225472 | bytes 23855104 | tf_op jit(solution)/shard_map/rjcf,jfd->rjcd/dot_general | solution.py:35
  167.2 9.5 %fusion.12 = bf16[32,2,6,4096]{3,0,2,1:T(8,128)(2,1)S(1)} fusion(f32[2,32,6,4096]{3,1,2,0:T(8,128)S(1)} %fusion, bf16[32,2,6,1024]{3,0,2,1:T(8,128)(2,1)S(1)} %get-tuple-element.4, bf16[2,1024,4096]{2,1,0:T(8,128)(2,1)} %param.16), kind=kOutput, calls=%fused_computation.14 | convolution fusion | flops 3224371200 | bytes 27000832 | tf_op jit(solution)/shard_map/rjcf,jfd->rjcd/dot_general | solution.py:36
  176.7 3.8 %copy.80 = bf16[32,2,6,4096]{3,2,1,0:T(8,128)(2,1)} copy(bf16[32,2,6,4096]{3,0,2,1:T(8,128)(2,1)S(1)} %fusion.12) | data formatting | bytes 6291456 | tf_op jit(solution)/shard_map/convert_element_type | solution.py:100
  180.5 4.2 %reshape.57 = bf16[2,4,48,4096]{3,2,1,0:T(8,128)(2,1)S(1)} reshape(bf16[32,2,6,4096]{3,2,1,0:T(8,128)(2,1)} %copy.80) | data formatting | bytes 6291456 | tf_op jit(solution)/shard_map/reshape | solution.py:102
  184.7 0.1 dynamic-slice_bitcast_fusion
  184.8 0.6 collective-permute-start.3
  185.4 1.1 copy-done.11
  186.6 11.0 %bitcast_convert_fusion = bf16[2,1024,4096]{2,1,0:T(8,128)(2,1)} fusion(bf16[32,2,6,4096]{3,1,2,0:T(2,128)(2,1)S(1)} %copy-done.11, f32[2,32,6,1024]{3,1,2,0:T(8,128)} %fusion.8, f32[2,32,6,1024]{3,1,2,0:T(8,128)} %fusion.2), kind=kOutput, calls=%fused_computation | convolution fusion | flops 3231973376 | bytes 23068672 | tf_op jit(solution)/shard_map/rjcf,rjcd->jfd/dot_general | solution.py:30
  197.6 21.6 %collective-permute-done.3 = bf16[4,48,4096]{2,1,0:T(8,128)(2,1)S(1)} collective-permute-done((bf16[4,48,4096]{2,1,0:T(8,128)(2,1)S(1)}, bf16[4,48,4096]{2,1,0:T(8,128)(2,1)S(1)}, u32[]{:S(2)}, u32[]{:S(2)}) %collective-permute-start.3) | collective-permute-done | bytes 1572896 | tf_op jit(solution)/shard_map/ppermute | solution.py:47
  219.2 0.5 fusion.16
  219.8 0.0 copy-start.2
  219.8 1.1 copy-done.2
  220.9 0.1 dynamic-slice_bitcast_fusion.3
  221.0 1.8 collective-permute-start.4
  222.9 2.3 collective-permute-start.6
  225.1 1.0 collective-permute-start.5
  226.1 13.5 %bitcast_convert_fusion.1 = bf16[2,1024,4096]{2,1,0:T(8,128)(2,1)} fusion(bf16[32,2,6,1024]{3,0,2,1:T(8,128)(2,1)} %copy-done.5, bf16[32,2,6,4096]{3,1,2,0:T(2,128)(2,1)} %all-gather.5.cloned.1.call-done), kind=kOutput, calls=%fused_computation.1 | convolution fusion | flops 3229614080 | bytes 20709376 | tf_op jit(solution)/shard_map/rjcf,rjcd->jfd/dot_general | solution.py:29
  239.6 1.2 collective-permute-done.6
  240.8 17.0 %collective-permute-done.5 = bf16[48,4096]{1,0:T(8,128)(2,1)S(1)} collective-permute-done((bf16[48,4096]{1,0:T(8,128)(2,1)S(1)}, bf16[48,4096]{1,0:T(8,128)(2,1)S(1)}, u32[]{:S(2)}, u32[]{:S(2)}) %collective-permute-start.5) | collective-permute-done | bytes 393248 | tf_op jit(solution)/shard_map/ppermute | solution.py:47
  257.8 1.2 fusion.35
  259.0 0.1 reshape.58
  259.2 1.2 copy.81
  260.3 3.5 %all-to-all-start.2 = ((bf16[4,2,6,4096]{3,1,2,0:T(2,128)(2,1)}), bf16[4,2,6,4096]{3,1,2,0:T(2,128)(2,1)S(1)}, u32[]{:S(2)}, u32[]{:S(2)}) async-start(bf16[4,2,6,4096]{3,1,2,0:T(2,128)(2,1)} %copy.81), calls=%async_computation.2 | async-start | bytes 786432 | tf_op jit(solution)/shard_map/all_to_all | solution.py:104
  263.8 0.0 copy-start.8
  263.8 14.7 %bitcast_convert_fusion.2 = bf16[2,1024,4096]{2,1,0:T(8,128)(2,1)} fusion(bf16[32,2,6,1024]{3,0,2,1:T(8,128)(2,1)S(1)} %copy-done.4, bf16[32,2,6,4096]{3,1,2,0:T(2,128)(2,1)} %all-gather.5.cloned.1.call-done), kind=kOutput, calls=%fused_computation.2 | convolution fusion | flops 3229614080 | bytes 20709376 | tf_op jit(solution)/shard_map/rjcf,rjcd->jfd/dot_general | solution.py:28
  278.5 0.2 copy.82
  278.7 0.1 reshape.59
  278.9 0.9 convolution_convert_fusion.1
  (25 shorter events, 0.1 us)
Async XLA Ops:
  7.2 2.5 copy-start
  7.2 29.7 %copy-start.9 = (f32[20,2]{0,1:T(2,128)S(1)}, f32[20,2]{0,1:T(2,128)}, u32[]{:S(2)}) copy-start(f32[20,2]{0,1:T(2,128)} %param.12) | copy-start | bytes 484
  7.2 30.0 %copy-start.6 = (bf16[20,4096]{1,0:T(8,128)(2,1)S(1)}, bf16[20,4096]{1,0:T(8,128)(2,1)}, u32[]{:S(2)}) copy-start(bf16[20,4096]{1,0:T(8,128)(2,1)} %param.10) | copy-start | bytes 491524
  7.2 75.8 %all-gather.5.cloned.1.call-start = ((), (), s32[]{:S(2)}) async-start(), calls=%async_computation.4 | async-start | bytes 3538944 | tf_op jit(solution)/shard_map/all_gather | solution.py:93
  9.7 38.9 %copy-start.7 = (bf16[20,48]{1,0:T(8,128)(2,1)}, bf16[20,48]{1,0:T(8,128)(2,1)S(1)}, u32[]{:S(2)}) copy-start(bf16[20,48]{1,0:T(8,128)(2,1)S(1)} %fusion.36) | copy-start | bytes 5764
  22.1 121.7 %all-gather.3.cloned.1.call-start = ((), (), s32[]{:S(2)}) async-start(), calls=%async_computation.3 | async-start | bytes 3538944 | tf_op jit(solution)/shard_map/all_gather | solution.py:94
  22.8 13.3 %collective-permute-start.2 = (f32[1,1]{1,0:T(1,128)}, f32[1,1]{1,0:T(1,128)}, u32[]{:S(2)}, u32[]{:S(2)}) collective-permute-start(f32[1,1]{1,0:T(1,128)} %mul.63), channel_id=1, source_target_pairs={{0,3},{1,0},{2,1},{3,2},{4,7},{5,4},{6,5},{7,6},{8,11},{9,8},{10,9... | collective-permute-start | bytes 20 | tf_op jit(solution)/shard_map/ppermute | solution.py:57
  28.2 7.3 %collective-permute-start.1 = (f32[1,1]{1,0:T(1,128)}, f32[1,1]{1,0:T(1,128)}, u32[]{:S(2)}, u32[]{:S(2)}) collective-permute-start(f32[1,1]{1,0:T(1,128)} %mul.63), channel_id=1, source_target_pairs={{0,2},{1,3},{2,0},{3,1},{4,6},{5,7},{6,4},{7,5},{8,10},{9,11},{10,... | collective-permute-start | bytes 20 | tf_op jit(solution)/shard_map/ppermute | solution.py:57
  29.5 5.5 %collective-permute-start = (f32[1,1]{1,0:T(1,128)}, f32[1,1]{1,0:T(1,128)}, u32[]{:S(2)}, u32[]{:S(2)}) collective-permute-start(f32[1,1]{1,0:T(1,128)} %mul.63), channel_id=1, source_target_pairs={{0,1},{1,2},{2,3},{3,0},{4,5},{5,6},{6,7},{7,4},{8,9},{9,10},{10,1... | collective-permute-start | bytes 20 | tf_op jit(solution)/shard_map/ppermute | solution.py:57
  83.0 15.3 %copy-start.10 = (bf16[32,2,6,4096]{3,1,2,0:T(2,128)(2,1)S(1)}, bf16[32,2,6,4096]{3,1,2,0:T(2,128)(2,1)}, u32[]{:S(2)}) copy-start(bf16[32,2,6,4096]{3,1,2,0:T(2,128)(2,1)} %all-gather.5.cloned.1.call-done) | copy-start | bytes 9437188
  158.8 8.4 %copy-start.3 = (bf16[32,2,6,1024]{3,0,2,1:T(8,128)(2,1)}, bf16[32,2,6,1024]{3,0,2,1:T(8,128)(2,1)S(1)}, u32[]{:S(2)}) copy-start(bf16[32,2,6,1024]{3,0,2,1:T(8,128)(2,1)S(1)} %get-tuple-element.5) | copy-start | bytes 2359300
  158.8 8.4 %copy-start.5 = (bf16[32,2,6,1024]{3,0,2,1:T(8,128)(2,1)}, bf16[32,2,6,1024]{3,0,2,1:T(8,128)(2,1)S(1)}, u32[]{:S(2)}) copy-start(bf16[32,2,6,1024]{3,0,2,1:T(8,128)(2,1)S(1)} %get-tuple-element.4) | copy-start | bytes 2359300
  184.7 1.9 copy-start.11
  184.8 34.4 %collective-permute-start.3 = (bf16[4,48,4096]{2,1,0:T(8,128)(2,1)S(1)}, bf16[4,48,4096]{2,1,0:T(8,128)(2,1)S(1)}, u32[]{:S(2)}, u32[]{:S(2)}) collective-permute-start(bf16[4,48,4096]{2,1,0:T(8,128)(2,1)S(1)} %dynamic-slice_bitcast_fusion), channel_id=1, source_target_pairs={{0,16},{16,0},{1,17},{17,1},{2,18},{18,2},{3,19},{19,3},{4,20},{20... | collective-permute-start | bytes 4718600 | tf_op jit(solution)/shard_map/ppermute | solution.py:47
  219.8 1.1 copy-start.2
  221.0 18.6 %collective-permute-start.4 = (bf16[48,4096]{1,0:T(8,128)(2,1)S(1)}, bf16[48,4096]{1,0:T(8,128)(2,1)S(1)}, u32[]{:S(2)}, u32[]{:S(2)}) collective-permute-start(bf16[48,4096]{1,0:T(8,128)(2,1)S(1)} %get-tuple-element.6), channel_id=1, source_target_pairs={{0,1},{1,2},{2,3},{3,0},{4,5},{5,6},{6,7},{7,4},{8,9},{9,10},{10,1... | collective-permute-start | bytes 1179656 | tf_op jit(solution)/shard_map/ppermute | solution.py:47
  222.9 18.0 %collective-permute-start.6 = (bf16[48,4096]{1,0:T(8,128)(2,1)S(1)}, bf16[48,4096]{1,0:T(8,128)(2,1)S(1)}, u32[]{:S(2)}, u32[]{:S(2)}) collective-permute-start(bf16[48,4096]{1,0:T(8,128)(2,1)S(1)} %get-tuple-element.7), channel_id=1, source_target_pairs={{0,3},{1,0},{2,1},{3,2},{4,7},{5,4},{6,5},{7,6},{8,11},{9,8},{10,9... | collective-permute-start | bytes 1179656 | tf_op jit(solution)/shard_map/ppermute | solution.py:47
  225.1 32.7 %collective-permute-start.5 = (bf16[48,4096]{1,0:T(8,128)(2,1)S(1)}, bf16[48,4096]{1,0:T(8,128)(2,1)S(1)}, u32[]{:S(2)}, u32[]{:S(2)}) collective-permute-start(bf16[48,4096]{1,0:T(8,128)(2,1)S(1)} %get-tuple-element.8), channel_id=1, source_target_pairs={{0,2},{1,3},{2,0},{3,1},{4,6},{5,7},{6,4},{7,5},{8,10},{9,11},{10,... | collective-permute-start | bytes 1179656 | tf_op jit(solution)/shard_map/ppermute | solution.py:47
  239.6 24.2 %copy-start.4 = (bf16[32,2,6,1024]{3,0,2,1:T(8,128)(2,1)S(1)}, bf16[32,2,6,1024]{3,0,2,1:T(8,128)(2,1)}, u32[]{:S(2)}) copy-start(bf16[32,2,6,1024]{3,0,2,1:T(8,128)(2,1)} %copy-done.3) | copy-start | bytes 2359300
  260.3 18.2 %all-to-all-start.2 = ((bf16[4,2,6,4096]{3,1,2,0:T(2,128)(2,1)}), bf16[4,2,6,4096]{3,1,2,0:T(2,128)(2,1)S(1)}, u32[]{:S(2)}, u32[]{:S(2)}) async-start(bf16[4,2,6,4096]{3,1,2,0:T(2,128)(2,1)} %copy.81), calls=%async_computation.2 | async-start | bytes 786432 | tf_op jit(solution)/shard_map/all_to_all | solution.py:104
  263.8 15.1 %copy-start.8 = (bf16[20,48]{1,0:T(8,128)(2,1)S(1)}, bf16[20,48]{1,0:T(8,128)(2,1)}, u32[]{:S(2)}) copy-start(bf16[20,48]{1,0:T(8,128)(2,1)} %copy-done.7) | copy-start | bytes 5764
  263.8 15.9 %copy-start.1 = (bf16[20,4096]{1,0:T(8,128)(2,1)S(1)}, bf16[20,4096]{1,0:T(8,128)(2,1)}, u32[]{:S(2)}) copy-start(bf16[20,4096]{1,0:T(8,128)(2,1)} %param.9) | copy-start | bytes 491524
Sparse Core Ops, SparseCore 0:
  22.3 60.6 all-gather.4
  85.1 58.6 all-gather.2
where the time goes:
time: 290 us; the launch traced here: 287 us
  waiting for transfers between devices  108 us (37%)
  matrix products  103 us (36%)
  blocking collectives  22.1 us (8%)
  starting transfers between devices  18.2 us (6%)
  between operations  17.9 us (6%)
  local copies, waits for them, and re-layouts  14.7 us (5%)
  other arithmetic  2.96 us (1%)
    ppermute x4, waiting for transfers between devices, send_sum(): total = total + lax.ppermute(outgoing, axis, perm).astype(jnp.float32)  39.8 us
    all_gather x1, waiting for transfers between devices, local(): lax.all_gather(arrived_inputs, ('dp', 'sample'), axis=0, tiled=True)  34.4 us
    all_gather x1, waiting for transfers between devices, local(): lax.all_gather(arrived_grads, ('dp', 'sample'), axis=0, tiled=True)  31 us
    dot_general x1, matrix products, expert_rows(): jnp.einsum('rjcd,jfd->rjcf', inputs, w_gate, preferred_element_type=jnp.f...  15.3 us
    dot_general x1, matrix products, expert_rows(): jnp.einsum('rjcd,jfd->rjcf', grads_out, w_down, preferred_element_type=jn...  15 us
    dot_general x1, matrix products, weight_terms(): jnp.einsum('rjcf,rjcd->jfd', grad_gate, inputs, preferred_element_type=jn...  14.7 us
    dot_general x1, matrix products, expert_rows(): jnp.einsum('rjcd,jfd->rjcf', inputs, w_up, preferred_element_type=jnp.flo...  14.6 us
    dot_general x1, matrix products, weight_terms(): jnp.einsum('rjcf,rjcd->jfd', grad_up, inputs, preferred_element_type=jnp....  13.5 us
  transfers between devices with their start and end apart: 10, of which 6 were waited for; matrix products, arithmetic and copies ran while one was open for 24% of the time, Pallas kernels for 0%

commit v1 on v0

--- a/solution.py
+++ b/solution.py
@@ -1,9 +1,16 @@
+import functools
+
 import jax
 import jax.numpy as jnp
 from jax import lax
+from jax.experimental import pallas as pl
+from jax.experimental.pallas import tpu as pltpu
 from jax.sharding import PartitionSpec as P
 
 CAP = 6
+BF16 = jnp.bfloat16
+F32 = jnp.float32
+MESH = pl.DeviceIdType.MESH
 
 
 def silu_parts(pre_gate):
@@ -114,6 +121,554 @@
     )
 
 
+NSUB = 4
+NQ = 4
+LANES = 128
+
+
+def dot_nt(a, b):
+    return lax.dot_general(a, b, (((1,), (1,)), ((), ())), preferred_element_type=F32)
+
+
+def dot_nn(a, b):
+    return lax.dot_general(a, b, (((1,), (0,)), ((), ())), preferred_element_type=F32)
+
+
+def eye(n):
+    rows = lax.broadcasted_iota(jnp.int32, (n, n), 0)
+    cols = lax.broadcasted_iota(jnp.int32, (n, n), 1)
+    return jnp.where(rows == cols, 1.0, 0.0).astype(BF16)
+
+
+def pack_meta(routes, gate_weights, lengths, rewards, experts, per_group, ns, rows):
+    tokens = routes.shape[0]
+    z = lax.axis_index("sample")
+    ids = jnp.arange(experts, dtype=jnp.int32)
+    hit = routes[:, :, None] == ids[None, None, :]
+    member = jnp.any(hit, axis=1)
+    pos = jnp.arange(tokens, dtype=jnp.int32)
+    before = (pos[None, :] < pos[:, None])[:, :, None] & member[None, :, :]
+    rank = jnp.sum(before.astype(jnp.int32), axis=1)
+    live = (pos < lengths[0, 0]).astype(F32)
+    gate = jnp.sum(jnp.where(hit, gate_weights[:, :, None], 0.0), axis=1) * live[:, None]
+    cap_line = ns * CAP
+    slot = rank + (ids % per_group)[None, :] * cap_line + z * CAP + 1
+    sub = jnp.arange(NSUB, dtype=jnp.int32)[:, None, None] * (per_group * cap_line)
+    code = jnp.where(member[None], slot[None] + sub, 0).astype(F32)
+    gate = jnp.broadcast_to(gate[None], code.shape)
+
+    def lanes(a):
+        a = jnp.transpose(a, (2, 0, 1)).reshape(experts // per_group, per_group, rows)
+        return a
+
+    both = jnp.concatenate([lanes(code), lanes(gate)], axis=1)
+    both = both.reshape(-1, 4 * per_group, rows)
+    reward = jnp.broadcast_to(
+        rewards.astype(F32).reshape(1, 1, 1) * 0.0625, both.shape[:2] + (LANES - rows,)
+    )
+    return jnp.concatenate([both, reward], axis=2)
+
+
+def fused_kernel(
+    cfg,
+    tok, cot, meta, wg, wu, wd,
+    gt, h_out, gg_out, gu_out, x_out,
+    buf, mbuf, r0, r1, r2, r3, xs, xq, acc, ht, gn, sel, sel_t, scol, wslot,
+    z_send, z_recv, l_send, l_recv, d_recv, a_send, a_recv, b_send, b_recv,
+    c_send, c_recv, e_send, e_recv, wsem, osem,
+):
+    ns, rows, cw, m, h, jl, cap_line = (
+        cfg["ns"], cfg["rows"], cfg["cw"], cfg["m"], cfg["h"], cfg["jl"], cfg["cap_line"]
+    )
+    nk = 2 * NQ
+    cq = NSUB * cw
+    kl = ns * rows
+    x = lax.axis_index("dp")
+    ex = lax.axis_index("expert")
+    z = lax.axis_index("sample")
+    y = ex // 2
+    c = ex % 2
+    x1, y1 = x + (1 - c) * (1 - 2 * x), y + c * (1 - 2 * y)
+    x2, y2 = x + c * (1 - 2 * x), y + (1 - c) * (1 - 2 * y)
+    l0 = x * 2 + y
+    l1 = x1 * 2 + y1
+    l2 = x2 * 2 + y2
+    l3 = (1 - x) * 2 + (1 - y)
+
+    def dev(xx, yy, cc, zz):
+        return {"dp": xx, "expert": yy * 2 + cc, "sample": zz}
+
+    d1, d2, dc = dev(x1, y1, c, z), dev(x2, y2, c, z), dev(x, y, 1 - c, z)
+
+    def zpeer(o):
+        return (z + o) % ns
+
+    def zsrc(o):
+        return (z - o + ns) % ns
+
+    barrier = pltpu.get_barrier_semaphore()
+    peers = [d1, d2, dc] + [dev(x, y, c, zpeer(o)) for o in range(1, ns)]
+    for p in peers:
+        pl.semaphore_signal(barrier, inc=1, device_id=p, device_id_type=MESH)
+
+    def load(mat, q, slot):
+        return pltpu.make_async_copy(
+            mat.at[:, :, pl.ds(pl.multiple_of(q * cq, cq), cq)], wslot.at[slot], wsem.at[slot]
+        )
+
+    load(wg, 0, 0).start()
+    load(wu, 0, 1).start()
+    load(wg, 1, 2).start()
+    load(wu, 1, 3).start()
+    load(wd, 0, 4).start()
+    load(wd, 1, 5).start()
+
+    for q in range(NQ):
+        buf[q, c, l0, z] = tok[q]
+        buf[NQ + q, c, l0, z] = cot[q]
+    mbuf[c, l0, z] = meta[...]
+    acc[...] = jnp.zeros_like(acc)
+    pl.semaphore_wait(barrier, len(peers))
+
+    def rc(src, dst, s, r, to):
+        return pltpu.make_async_remote_copy(
+            src_ref=src, dst_ref=dst, send_sem=s, recv_sem=r, device_id=to, device_id_type=MESH
+        )
+
+    def slab(k):
+        return mbuf if isinstance(k, int) and k == nk else buf.at[k]
+
+    def src_of(k):
+        if isinstance(k, int) and k == nk:
+            return meta
+        return tok.at[k] if k < NQ else cot.at[k - NQ]
+
+    def z_copy(k, o):
+        to = dev(x, y, c, zpeer(o))
+        return rc(src_of(k), slab(k).at[c, l0, z], z_send.at[k, o], z_recv.at[k, o], to)
+
+    def z_wait(k):
+        for o in range(1, ns):
+            b = slab(k).at[c, l0, zsrc(o)]
+            rc(b, b, z_send.at[k, o], z_recv.at[k, o], d1).wait_recv()
+
+    def line(k, cc, ll, si, r, to):
+        b = slab(k).at[cc, ll]
+        return rc(b, b, l_send.at[k, si], r, to)
+
+    def stage_a(k):
+        z_wait(k)
+        line(k, c, l0, 0, l_recv.at[k, 0], d1).start()
+        line(k, c, l0, 1, l_recv.at[k, 1], d2).start()
+        line(k, c, l0, 2, d_recv.at[k, l0], dc).start()
+
+    def stage_b(k):
+        line(k, c, l1, 0, l_recv.at[k, 0], d1).wait_recv()
+        line(k, c, l1, 3, l_recv.at[k, 2], d2).start()
+        line(k, c, l1, 4, d_recv.at[k, l1], dc).start()
+
+    def stage_c(k):
+        line(k, c, l2, 1, l_recv.at[k, 1], d2).wait_recv()
+        line(k, c, l2, 5, d_recv.at[k, l2], dc).start()
+        line(k, c, l3, 3, l_recv.at[k, 2], d2).wait_recv()
+        line(k, c, l3, 6, d_recv.at[k, l3], dc).start()
+
+    def stage_d(k):
+        for ll in range(4):
+            line(k, 1 - c, ll, 2, d_recv.at[k, ll], dc).wait_recv()
+
+    def drain(k):
+        for i in range(7):
+            line(k, c, l0, i, l_recv.at[k, 0], d1).wait_send()
+
+    for k in [nk] + list(range(nk)):
+        for o in range(1, ns):
+            z_copy(k, o).start()
+
+    def build(g):
+        mz = [mbuf[g // 4, g % 4, zz, ex // 2] for zz in range(ns)]
+        lane = lax.broadcasted_iota(jnp.int32, (4 * jl, LANES), 1)
+        rew = [
+            jnp.sum(jnp.where(lane == LANES - 1, b, 0.0), axis=1, keepdims=True) for b in mz
+        ]
+        total = rew[0]
+        for r in rew[1:]:
+            total = total + r
+        wide = -(-kl // LANES) * LANES
+        vec = jnp.zeros((2 * jl, wide), F32)
+        for zz in range(ns):
+            adv = rew[zz] - (total - rew[zz]) / (ns - 1)
+            b = jnp.where(lane < rows, mz[zz], 0.0)
+            b = jnp.where(c == 1, b[2 * jl :], b[: 2 * jl])
+            kind = lax.broadcasted_iota(jnp.int32, (2 * jl, LANES), 0)
+            b = jnp.where(kind >= jl, b * (-adv[: 2 * jl]), b)
+            b = jnp.concatenate([b, jnp.zeros((2 * jl, wide - LANES), F32)], axis=1)
+            vec = vec + (pltpu.roll(b, zz * rows, 1) if zz else b)
+        vec = vec[:, :kl]
+        slots = NSUB * jl * cap_line
+        ids = lax.broadcasted_iota(jnp.int32, (slots, kl), 0).astype(F32) + 1.0
+        one = jnp.zeros((slots, kl), F32)
+        scale = jnp.zeros((slots, kl), F32)
+        for j in range(jl):
+            same = ids == vec[j : j + 1]
+            one = jnp.where(same, 1.0, one)
+            scale = jnp.where(same, vec[jl + j : jl + j + 1], scale)
+        one = one.astype(BF16)
+        sel[g] = one
+        scol[g] = jnp.sum(scale, axis=1, keepdims=True)
+        sel_t[g] = dot_nt(eye(kl), one).astype(BF16)
+
+    def select(k, scaled):
+        def body(g, _):
+            rowsv = buf[k, g // 4, g % 4].reshape(kl, cw)
+            out = dot_nn(sel[g], rowsv)
+            if scaled:
+                out = out * scol[g]
+            at = pl.ds(pl.multiple_of(g * cap_line, cap_line), cap_line)
+            for s in range(NSUB):
+                for j in range(jl):
+                    r = (s * jl + j) * cap_line
+                    xq[j, at, s * cw : (s + 1) * cw] = out[r : r + cap_line]
+            return 0
+
+        lax.fori_loop(0, 8, body, 0)
+        xs[k] = xq[...].astype(BF16)
+
+    def accumulate(i, slot, k):
+        half = h // 2
+
+        def body(t, _):
+            j = t // 2
+            r = pl.ds(pl.multiple_of((t % 2) * half, half), half)
+            acc[i, j, r] += dot_nt(wslot[slot, j, r], xs[k, j])
+            return 0
+
+        lax.fori_loop(0, 2 * jl, body, 0)
+
+    def wait_w(slot):
+        load(wg, 0, slot).wait()
+
+    def step(i):
+        @pl.when(i < nk)
+        def _():
+            stage_a(i)
+
+        @pl.when((i >= 1) & (i < nk + 1))
+        def _():
+            stage_b(i - 1)
+
+        @pl.when((i >= 2) & (i < nk + 2))
+        def _():
+            stage_c(i - 2)
+
+        @pl.when(i >= 3)
+        def _():
+            stage_d(i - 3)
+
+    stage_a(nk)
+    step(0)
+    stage_b(nk)
+    step(1)
+    stage_c(nk)
+    step(2)
+    stage_d(nk)
+    lax.fori_loop(0, 8, lambda g, _: (build(g), 0)[1], 0)
+
+    def token_chunk(q, _):
+        step(q + 3)
+        select(q, False)
+        s = 2 * (q % 2)
+        wait_w(s)
+        accumulate(0, s, q)
+        wait_w(s + 1)
+        accumulate(1, s + 1, q)
+
+        @pl.when(q < NQ - 2)
+        def _():
+            load(wg, q + 2, s).start()
+            load(wu, q + 2, s + 1).start()
+
+        return 0
+
+    lax.fori_loop(0, NQ, token_chunk, 0)
+
+    def cot_chunk(q, _):
+        step(q + NQ + 3)
+        select(q + NQ, True)
+        s = 4 + q % 2
+        wait_w(s)
+        accumulate(2, s, q + NQ)
+
+        @pl.when(q < NQ - 2)
+        def _():
+            load(wd, q + 2, s).start()
+
+        @pl.when(q == NQ - 2)
+        def _():
+            load(wg, 1, s).start()
+
+        @pl.when(q == NQ - 1)
+        def _():
+            load(wu, 1, s).start()
+
+        return 0
+
+    lax.fori_loop(0, NQ, cot_chunk, 0)
+
+    def finish(t, _):
+        tile = h // 4
+        j = t // 4
+        r = pl.ds(pl.multiple_of((t % 4) * tile, tile), tile)
+        g, u, gh = acc[0, j, r], acc[1, j, r], acc[2, j, r]
+        act, der = silu_parts(g)
+        ht[0, j, r] = (act * u).astype(BF16)
+        ht[1, j, r] = (gh * u * der).astype(BF16)
+        ht[2, j, r] = (gh * act).astype(BF16)
+        return 0
+
+    lax.fori_loop(0, 4 * jl, finish, 0)
+
+    def turn(t, _):
+        gn[t // jl, t % jl] = dot_nt(eye(m), ht[1 + t // jl, t % jl]).astype(BF16)
+        return 0
+
+    lax.fori_loop(0, 2 * jl, turn, 0)
+    outs = [
+        pltpu.make_async_copy(ht.at[0], h_out, osem.at[0]),
+        pltpu.make_async_copy(ht.at[1], gg_out, osem.at[1]),
+        pltpu.make_async_copy(ht.at[2], gu_out, osem.at[2]),
+        pltpu.make_async_copy(xs, x_out, osem.at[3]),
+    ]
+    for o in outs:
+        o.start()
+
+    def drain_all(k, _):
+        drain(k)
+        return 0
+
+    lax.fori_loop(0, nk, drain_all, 0)
+    drain(nk)
+
+    def parts(i):
+        q = NQ - 1 - i
+        s = (2 - 2 * i + 12) % 6
+
+        @pl.when(i >= 2)
+        def _():
+            wait_w(s)
+            wait_w(s + 1)
+
+        def body(j, _):
+            xq[j] = dot_nn(gn[0, j], wslot[s, j]) + dot_nn(gn[1, j], wslot[s + 1, j])
+            return 0
+
+        lax.fori_loop(0, jl, body, 0)
+
+        @pl.when(i == 0)
+        def _():
+            load(wg, 0, s).start()
+            load(wu, 0, s + 1).start()
+
+        def back(g, _):
+            at = pl.ds(pl.multiple_of(g * cap_line, cap_line), cap_line)
+            pieces = [
+                xq[j, at, sb * cw : (sb + 1) * cw] for sb in range(NSUB) for j in range(jl)
+            ]
+            v = jnp.concatenate(pieces, axis=0).astype(BF16)
+            o = dot_nn(sel_t[g], v).astype(BF16)
+            buf[q, g // 4, g % 4] = o.reshape(ns, rows, cw)
+            return 0
+
+        lax.fori_loop(0, 8, back, 0)
+        send_core(q).start()
+
+    def send_core(q):
+        return rc(buf.at[q, 1 - c], r0.at[q], a_send.at[q], a_recv.at[q], dc)
+
+    def send_far(q, i):
+        return rc(
+            buf.at[q, c, (l2, l3)[i]], r1.at[q, i], b_send.at[q, i], b_recv.at[q, i], d2
+        )
+
+    def send_near(q):
+        return rc(buf.at[q, c, l1], r2.at[q], c_send.at[q], c_recv.at[q], d1)
+
+    def send_z(q, o):
+        to = dev(x, y, c, zpeer(o))
+        return rc(buf.at[q, c, l0, zpeer(o)], r3.at[q, o], e_send.at[q, o], e_recv.at[q, o], to)
+
+    def s1(q):
+        send_core(q).wait_recv()
+        for i, ll in ((0, l2), (1, l3)):
+            buf[q, c, ll] = (buf[q, c, ll].astype(F32) + r0[q, ll].astype(F32)).astype(BF16)
+            send_far(q, i).start()
+        for ll in (l0, l1):
+            buf[q, c, ll] = (buf[q, c, ll].astype(F32) + r0[q, ll].astype(F32)).astype(BF16)
+
+    def s2(q):
+        send_far(q, 1).wait_recv()
+        buf[q, c, l1] = (buf[q, c, l1].astype(F32) + r1[q, 1].astype(F32)).astype(BF16)
+        send_near(q).start()
+        send_far(q, 0).wait_recv()
+        buf[q, c, l0] = (buf[q, c, l0].astype(F32) + r1[q, 0].astype(F32)).astype(BF16)
+
+    def s3(q):
+        send_near(q).wait_recv()
+        buf[q, c, l0] = (buf[q, c, l0].astype(F32) + r2[q].astype(F32)).astype(BF16)
+        for o in range(1, ns):
+            send_z(q, o).start()
+
+    def s4(q):
+        total = buf[q, c, l0, z].astype(F32)
+        for o in range(1, ns):
+            send_z(q, o).wait_recv()
+            total = total + r3[q, o].astype(F32)
+        gt[q] = total.astype(BF16)
+
+    lags = cfg["lags"]
+
+    def back_step(i, _):
+        @pl.when(i < NQ)
+        def _():
+            parts(i)
+
+        for fn, lag in zip((s1, s2, s3, s4), lags):
+
+            @pl.when((i >= lag) & (i < lag + NQ))
+            def _():
+                fn(NQ - 1 - (i - lag))
+
+        return 0
+
+    lax.fori_loop(0, NQ + lags[-1], back_step, 0)
+
+    def finish_sends(q, _):
+        send_core(q).wait_send()
+        send_far(q, 0).wait_send()
+        send_far(q, 1).wait_send()
+        send_near(q).wait_send()
+        for o in range(1, ns):
+            send_z(q, o).wait_send()
+        return 0
+
+    lax.fori_loop(0, NQ, finish_sends, 0)
+    for k in [nk] + list(range(nk)):
+        for o in range(1, ns):
+            z_copy(k, o).wait_send()
+    for o in outs:
+        o.wait()
+
+
+def weight_kernel(ht, gg, gu, xr, gr, o_gate, o_up, o_down):
+    o_gate[0] = dot_nn(gg[0], xr[0, 0]).astype(BF16)
+    o_up[0] = dot_nn(gu[0], xr[0, 0]).astype(BF16)
+    o_down[0] = dot_nn(ht[0], gr[0, 0]).astype(BF16)
+
+
+def fused(tokens, cotangent, routes, gate_weights, lengths, rewards, w_gate, w_up, w_down):
+    ns = lax.axis_size("sample")
+    t, d = tokens.shape
+    jl, h, _ = w_gate.shape
+    experts = jl * lax.axis_size("expert")
+    rows = NSUB * t
+    cw = d // (NSUB * NQ)
+    cq = NSUB * cw
+    cap_line = ns * CAP
+    lines = 4
+    m = 2 * lines * cap_line
+    nk = 2 * NQ
+    kl = ns * rows
+    slots = NSUB * jl * cap_line
+    cfg = dict(
+        ns=ns, rows=rows, cw=cw, m=m, h=h, jl=jl, cap_line=cap_line, lags=(1, 3, 4, 6)
+    )
+
+    def fold(a):
+        return a.reshape(t, NQ, NSUB, cw).transpose(1, 2, 0, 3).reshape(NQ, rows, cw)
+
+    meta = pack_meta(routes, gate_weights, lengths, rewards, experts, jl, ns, rows)
+    vmem = pl.BlockSpec(memory_space=pltpu.VMEM)
+    hbm = pl.BlockSpec(memory_space=pltpu.HBM)
+    dma = pltpu.SemaphoreType.DMA
+    block = (rows, cw)
+    back, ht, gg, gu, xs = pl.pallas_call(
+        functools.partial(fused_kernel, cfg),
+        name="gather_experts_scatter",
+        out_shape=(
+            jax.ShapeDtypeStruct((NQ,) + block, BF16),
+            jax.ShapeDtypeStruct((jl, h, m), BF16),
+            jax.ShapeDtypeStruct((jl, h, m), BF16),
+            jax.ShapeDtypeStruct((jl, h, m), BF16),
+            jax.ShapeDtypeStruct((nk, jl, m, cq), BF16),
+        ),
+        in_specs=[vmem] * 3 + [hbm] * 3,
+        out_specs=(vmem, hbm, hbm, hbm, hbm),
+        scratch_shapes=[
+            pltpu.VMEM((nk, 2, lines, ns) + block, BF16),
+            pltpu.VMEM((2, lines, ns) + meta.shape, F32),
+            pltpu.VMEM((NQ, lines, ns) + block, BF16),
+            pltpu.VMEM((NQ, 2, ns) + block, BF16),
+            pltpu.VMEM((NQ, ns) + block, BF16),
+            pltpu.VMEM((NQ, ns) + block, BF16),
+            pltpu.VMEM((nk, jl, m, cq), BF16),
+            pltpu.VMEM((jl, m, cq), F32),
+            pltpu.VMEM((3, jl, h, m), F32),
+            pltpu.VMEM((3, jl, h, m), BF16),
+            pltpu.VMEM((2, jl, m, h), BF16),
+            pltpu.VMEM((2 * lines, slots, kl), BF16),
+            pltpu.VMEM((2 * lines, kl, slots), BF16),
+            pltpu.VMEM((2 * lines, slots, 1), F32),
+            pltpu.VMEM((6, jl, h, cq), BF16),
+            dma((nk + 1, ns)), dma((nk + 1, ns)), dma((nk + 1, 7)), dma((nk + 1, 3)),
+            dma((nk + 1, 4)), dma((NQ,)), dma((NQ,)), dma((NQ, 2)), dma((NQ, 2)),
+            dma((NQ,)), dma((NQ,)), dma((NQ, ns)), dma((NQ, ns)), dma((6,)), dma((4,)),
+        ],
+        compiler_params=pltpu.CompilerParams(
+            collective_id=0, has_side_effects=True, vmem_limit_bytes=67043328
+        ),
+    )(fold(tokens), fold(cotangent), meta, w_gate, w_up, w_down)
+
+    full = pl.BlockSpec((1, h, m), lambda j, q: (j, 0, 0))
+    out = pl.BlockSpec((1, h, cq), lambda j, q: (j, 0, q))
+    shape = jax.ShapeDtypeStruct(w_gate.shape, BF16)
+    g_gate, g_up, g_down = pl.pallas_call(
+        weight_kernel,
+        name="weight_grads",
+        grid=(jl, NQ),
+        out_shape=(shape, shape, shape),
+        in_specs=[
+            full, full, full,
+            pl.BlockSpec((1, 1, m, cq), lambda j, q: (q, j, 0, 0)),
+            pl.BlockSpec((1, 1, m, cq), lambda j, q: (NQ + q, j, 0, 0)),
+        ],
+        out_specs=(out, out, out),
+        compiler_params=pltpu.CompilerParams(vmem_limit_bytes=48 * 1024 * 1024),
+    )(ht, gg, gu, xs, xs)
+    grad_tokens = back.reshape(NQ, NSUB, t, cw).transpose(2, 0, 1, 3).reshape(t, d)
+    return grad_tokens, g_gate, g_up, g_down
+
+
+def covered(mesh, tokens_shape, w_shape, rewards_shape):
+    nx, ne, ns = (mesh.shape[a] for a in ("dp", "expert", "sample"))
+    t = tokens_shape[0] // (nx * ne * ns)
+    d = tokens_shape[1]
+    h = w_shape[1] // (nx * ns)
+    prompt_one = rewards_shape == (nx * ne, ns)
+    return (
+        nx == 2
+        and ne == 4
+        and w_shape[0] == 2 * ne
+        and prompt_one
+        and ns > 1
+        and (ns * CAP) % 8 == 0
+        and (NSUB * t) % 16 == 0
+        and NSUB * t < LANES
+        and d % (NSUB * NQ * LANES) == 0
+        and h % 1024 == 0
+        and ns * t * d * h <= 80 * 4096 * 1024
+    )
+
+
 def solution(mesh):
     in_specs = (
         P(("dp", "expert", "sample"), None),
@@ -132,4 +687,12 @@
         P("expert", ("dp", "sample"), None),
         P("expert", ("dp", "sample"), None),
     )
-    return jax.shard_map(local, mesh=mesh, in_specs=in_specs, out_specs=out_specs, check_vma=False)
+
+    def run(*args):
+        fits = covered(mesh, args[0].shape, args[6].shape, args[5].shape)
+        body = fused if fits else local
+        return jax.shard_map(
+            body, mesh=mesh, in_specs=in_specs, out_specs=out_specs, check_vma=False
+        )(*args)
+
+    return run

time: 290 us -> 155 us (0.53); the launches traced: 287 us -> 155 us
  Pallas kernels: 0 us -> 141 us
  waiting for transfers between devices: 108 us -> 0 us
  matrix products: 103 us -> 0 us
  blocking collectives: 22.1 us -> 0 us
  starting transfers between devices: 18.2 us -> 0 us
  between operations: 17.9 us -> 2.05 us
  local copies, waits for them, and re-layouts: 14.7 us -> 10.2 us
    pallas_call x0 -> x2, Pallas kernels: none -> 141 us  [the longest x1 120 us: fused(): pl.pallas_call(functools.partial(fused_kernel, cfg), name='gather_experts...]
    dot_general x11 -> x0, matrix products: 103 us -> none  [the longest x1 15.3 us: expert_rows(): jnp.einsum('rjcd,jfd->rjcf', inputs, w_gate, preferred_element_type=jnp.f...]
    all_gather x2 -> x0, waiting for transfers between devices: 65.3 us -> none  [the longest x1 34.4 us: local(): lax.all_gather(arrived_inputs, ('dp', 'sample'), axis=0, tiled=True)]
    ppermute x7 -> x0, waiting for transfers between devices: 42.3 us -> none  [the longest x4 39.8 us: send_sum(): total = total + lax.ppermute(outgoing, axis, perm).astype(jnp.float32)]
    all_to_all x2 -> x0, blocking collectives: 22.1 us -> none  [the longest x1 11.6 us: local(): lax.all_to_all(sent_inputs.reshape(layout), 'expert', split_axis=0, conca...]
    ppermute x7 -> x0, starting transfers between devices: 14.7 us -> none  [the longest x3 8.95 us: local(): reward_total = reward_total + lax.ppermute(own_reward, 'sample', perm)]
    convert_element_type x1 -> x0, local copies, waits for them, and re-layouts: 3.77 us -> none  [local(): parts = input_terms(grad_gate, grad_up, w_gate, w_up).astype(jnp.bfloat16)]
    all_to_all x1 -> x0, starting transfers between devices: 3.46 us -> none  [local(): lax.all_to_all(row_sums, 'expert', split_axis=0, concat_axis=0, tiled=True)]
  transfers between devices with their start and end apart: 10 -> 0, of which waited for: 6 -> 0; matrix products, arithmetic and copies ran while one was open for 24% -> 0% of each run, Pallas kernels for 0% -> 0%
where the time goes in v1:
time: 155 us
  Pallas kernels  141 us (91%)
  local copies, waits for them, and re-layouts  10.2 us (7%)
  between operations  2.05 us (1%)
  other arithmetic  1.87 us (1%)
    pallas_call x1, Pallas kernels, fused(): pl.pallas_call(functools.partial(fused_kernel, cfg), name='gather_experts...  120 us
    pallas_call x1, Pallas kernels, fused(): pl.pallas_call(weight_kernel, name='weight_grads', grid=(jl, NQ), out_sha...  20.2 us
    unnamed x6, local copies, waits for them, and re-layouts  3.67 us
    reshape x6, local copies, waits for them, and re-layouts, fold(): a.reshape(t, NQ, NSUB, cw).transpose(1, 2, 0, 3).reshape(NQ, rows, cw)  3.54 us

profile of v1, /device:TPU:0, one launch (start us, length us, event | category | flops | bytes accessed | tf_op | source)
XLA Modules:
  0.0 154.8 jit_solution(6065776148450847636)
XLA Ops:
  0.6 0.7 fusion
  1.3 0.4 convert_reduce_fusion
  1.8 0.1 copy.38
  1.9 0.1 add.82
  2.0 0.1 broadcast_in_dim.34
  2.1 0.1 add.83
  2.1 0.1 add.84
  2.2 0.7 select_reduce_fusion
  3.6 0.1 reshape.114
  4.4 0.6 concatenate.7.meta
  5.0 1.0 reshape.110
  6.0 0.1 copy.36
  6.1 0.7 copy.39.tok
  6.8 1.0 reshape.112
  7.8 0.1 copy.37
  7.9 0.7 copy.40.cot
  8.6 120.4 %gather_experts_scatter.1 = (bf16[4,80,256]{2,1,0:T(8,128)(2,1)}, bf16[2,1024,192]{2,1,0:T(8,128)(2,1)}, bf16[2,1024,192]{2,1,0:T(8,128)(2,1)}, bf16[2,1024,192]{2,1,0:T(8,128)(2,1)}, bf16[8,2,192,1024]{3,2,1,0:T(8,128)(2,1)}) custom-call(bf16[4,80,256]{2,1,0:T(8,128)(2,1)} %copy.39.tok, bf16[4,80,256]{2,1,0:T(8,128)(2,1)} %copy.40.cot, ...), custom_call_target="tpu_custom_call" | custom-call | tf_op jit(solution)/shard_map/gather_experts_scatter/pallas_call | solution.py:594
  129.0 0.0 copy-start
  129.0 1.2 copy-done
  130.2 0.0 copy-start.1
  130.2 1.2 copy-done.1
  131.5 0.0 copy-start.2
  131.5 1.2 copy-done.2
  132.7 20.2 %weight_grads.1 = (bf16[2,1024,4096]{2,1,0:T(8,128)(2,1)}, bf16[2,1024,4096]{2,1,0:T(8,128)(2,1)}, bf16[2,1024,4096]{2,1,0:T(8,128)(2,1)}) custom-call(bf16[2,1024,192]{2,1,0:T(8,128)(2,1)S(1)} %copy-done, bf16[2,1024,192]{2,1,0:T(8,128)(2,1)S(1)} %copy-done.1, bf16[2,1024,192]{2,1,0:T(8,128)(2,1)S(1)} %copy-done.2, ...), custom_call_target="tpu_custom_call" | custom-call | tf_op jit(solution)/shard_map/weight_grads/pallas_call | solution.py:634
  152.9 1.0 copy.41
  153.9 0.1 copy.42
  154.0 0.8 reshape.117
  (11 shorter events, 0.1 us)
Async XLA Ops:
  129.0 1.2 copy-start
  130.2 1.2 copy-start.1
  131.5 1.2 copy-start.2

commit v2 on v1

--- a/solution.py
+++ b/solution.py
@@ -124,6 +124,8 @@
 NSUB = 4
 NQ = 4
 LANES = 128
+AHEAD = (2, 4, 5)
+LOOK = 2
 
 
 def dot_nt(a, b):
@@ -140,38 +142,49 @@
     return jnp.where(rows == cols, 1.0, 0.0).astype(BF16)
 
 
-def pack_meta(routes, gate_weights, lengths, rewards, experts, per_group, ns, rows):
-    tokens = routes.shape[0]
-    z = lax.axis_index("sample")
-    ids = jnp.arange(experts, dtype=jnp.int32)
-    hit = routes[:, :, None] == ids[None, None, :]
-    member = jnp.any(hit, axis=1)
-    pos = jnp.arange(tokens, dtype=jnp.int32)
-    before = (pos[None, :] < pos[:, None])[:, :, None] & member[None, :, :]
-    rank = jnp.sum(before.astype(jnp.int32), axis=1)
-    live = (pos < lengths[0, 0]).astype(F32)
-    gate = jnp.sum(jnp.where(hit, gate_weights[:, :, None], 0.0), axis=1) * live[:, None]
-    cap_line = ns * CAP
-    slot = rank + (ids % per_group)[None, :] * cap_line + z * CAP + 1
-    sub = jnp.arange(NSUB, dtype=jnp.int32)[:, None, None] * (per_group * cap_line)
-    code = jnp.where(member[None], slot[None] + sub, 0).astype(F32)
-    gate = jnp.broadcast_to(gate[None], code.shape)
-
-    def lanes(a):
-        a = jnp.transpose(a, (2, 0, 1)).reshape(experts // per_group, per_group, rows)
-        return a
-
-    both = jnp.concatenate([lanes(code), lanes(gate)], axis=1)
-    both = both.reshape(-1, 4 * per_group, rows)
-    reward = jnp.broadcast_to(
-        rewards.astype(F32).reshape(1, 1, 1) * 0.0625, both.shape[:2] + (LANES - rows,)
-    )
-    return jnp.concatenate([both, reward], axis=2)
+def pack_meta(routes, gate_weights, lengths, rewards, experts, jl, cap_line, z):
+    t = routes.shape[1]
+    eid = lax.broadcasted_iota(jnp.int32, (experts, t), 0)
+    live = lax.broadcasted_iota(jnp.int32, (1, t), 1) < lengths
+    member = jnp.zeros((experts, t), F32)
+    gate = jnp.zeros((experts, t), F32)
+    for k in range(routes.shape[0]):
+        hit = routes[k : k + 1] == eid
+        member = jnp.where(hit, 1.0, member)
+        gate = jnp.where(hit & live, gate_weights[k : k + 1], gate)
+    before = lax.broadcasted_iota(jnp.int32, (t, t), 0) < lax.broadcasted_iota(jnp.int32, (t, t), 1)
+    rank = dot_nn(member.astype(BF16), jnp.where(before, 1.0, 0.0).astype(BF16))
+    base = ((eid % jl) * cap_line + z * CAP + 1).astype(F32)
+    code = jnp.where(member > 0.0, rank + base, 0.0)
+    reward = rewards.astype(F32) * 0.0625
+    lanes = lax.broadcasted_iota(jnp.int32, (experts, LANES), 1)
+
+    def spread(a, step):
+        a = jnp.concatenate([a, jnp.zeros((experts, LANES - t), F32)], axis=1)
+        out = a
+        for sub in range(1, NSUB):
+            moved = pltpu.roll(a, sub * t, 1)
+            out = out + (jnp.where(moved > 0.0, moved + sub * step, 0.0) if step else moved)
+        return jnp.where(lanes == LANES - 1, reward, out)
+
+    return spread(code, float(jl * cap_line)), spread(gate, 0.0)
+
+
+def place(rows, t, sub):
+    r = lax.broadcasted_iota(jnp.int32, (rows, t), 0)
+    i = lax.broadcasted_iota(jnp.int32, (rows, t), 1)
+    return jnp.where(r == i + sub * t, 1.0, 0.0).astype(BF16)
+
+
+def take(rows, t, sub):
+    r = lax.broadcasted_iota(jnp.int32, (t, rows), 1)
+    i = lax.broadcasted_iota(jnp.int32, (t, rows), 0)
+    return jnp.where(r == i + sub * t, 1.0, 0.0).astype(BF16)
 
 
 def fused_kernel(
     cfg,
-    tok, cot, meta, wg, wu, wd,
+    tok, cot, routes, gates, lengths, rewards, wg, wu, wd,
     gt, h_out, gg_out, gu_out, x_out,
     buf, mbuf, r0, r1, r2, r3, xs, xq, acc, ht, gn, sel, sel_t, scol, wslot,
     z_send, z_recv, l_send, l_recv, d_recv, a_send, a_recv, b_send, b_recv,
@@ -223,11 +236,24 @@
     load(wd, 0, 4).start()
     load(wd, 1, 5).start()
 
-    for q in range(NQ):
-        buf[q, c, l0, z] = tok[q]
-        buf[NQ + q, c, l0, z] = cot[q]
-    mbuf[c, l0, z] = meta[...]
-    acc[...] = jnp.zeros_like(acc)
+    t = tok.shape[0]
+    spots = [place(rows, t, sub) for sub in range(NSUB)]
+
+    def fold(k):
+        ref, q = (tok, k) if k < NQ else (cot, k - NQ)
+        out = jnp.zeros((rows, cw), F32)
+        for sub in range(NSUB):
+            at = q * cq + sub * cw
+            out = out + dot_nn(spots[sub], ref[:, at : at + cw])
+        buf[k, c, l0, z] = out.astype(BF16)
+
+    code, gate = pack_meta(
+        routes[...], gates[...], lengths[...], rewards[...], mbuf.shape[4], jl, cap_line, z
+    )
+    mbuf[c, l0, z, 0] = code
+    mbuf[c, l0, z, 1] = gate
+    for k in range(LOOK):
+        fold(k)
     pl.semaphore_wait(barrier, len(peers))
 
     def rc(src, dst, s, r, to):
@@ -238,14 +264,13 @@
     def slab(k):
         return mbuf if isinstance(k, int) and k == nk else buf.at[k]
 
-    def src_of(k):
-        if isinstance(k, int) and k == nk:
-            return meta
-        return tok.at[k] if k < NQ else cot.at[k - NQ]
-
     def z_copy(k, o):
-        to = dev(x, y, c, zpeer(o))
-        return rc(src_of(k), slab(k).at[c, l0, z], z_send.at[k, o], z_recv.at[k, o], to)
+        b = slab(k).at[c, l0, z]
+        return rc(b, b, z_send.at[k, o], z_recv.at[k, o], dev(x, y, c, zpeer(o)))
+
+    def z_start(k):
+        for o in range(1, ns):
+            z_copy(k, o).start()
 
     def z_wait(k):
         for o in range(1, ns):
@@ -280,31 +305,40 @@
     def drain(k):
         for i in range(7):
             line(k, c, l0, i, l_recv.at[k, 0], d1).wait_send()
-
-    for k in [nk] + list(range(nk)):
         for o in range(1, ns):
-            z_copy(k, o).start()
+            z_copy(k, o).wait_send()
+
+    for k in list(range(LOOK)) + [nk]:
+        z_start(k)
+    for k in range(LOOK, nk):
+        fold(k)
+    acc[...] = jnp.zeros_like(acc)
 
     def build(g):
-        mz = [mbuf[g // 4, g % 4, zz, ex // 2] for zz in range(ns)]
-        lane = lax.broadcasted_iota(jnp.int32, (4 * jl, LANES), 1)
+        own = pl.ds(ex * jl, jl)
+        lane = lax.broadcasted_iota(jnp.int32, (jl, LANES), 1)
+        codes = [mbuf[g // 4, g % 4, zz, 0, own, :] for zz in range(ns)]
+        gates_z = [mbuf[g // 4, g % 4, zz, 1, own, :] for zz in range(ns)]
         rew = [
-            jnp.sum(jnp.where(lane == LANES - 1, b, 0.0), axis=1, keepdims=True) for b in mz
+            jnp.sum(jnp.where(lane == LANES - 1, b, 0.0), axis=1, keepdims=True) for b in codes
         ]
         total = rew[0]
         for r in rew[1:]:
             total = total + r
         wide = -(-kl // LANES) * LANES
-        vec = jnp.zeros((2 * jl, wide), F32)
-        for zz in range(ns):
-            adv = rew[zz] - (total - rew[zz]) / (ns - 1)
-            b = jnp.where(lane < rows, mz[zz], 0.0)
-            b = jnp.where(c == 1, b[2 * jl :], b[: 2 * jl])
-            kind = lax.broadcasted_iota(jnp.int32, (2 * jl, LANES), 0)
-            b = jnp.where(kind >= jl, b * (-adv[: 2 * jl]), b)
-            b = jnp.concatenate([b, jnp.zeros((2 * jl, wide - LANES), F32)], axis=1)
-            vec = vec + (pltpu.roll(b, zz * rows, 1) if zz else b)
-        vec = vec[:, :kl]
+
+        def along(blocks):
+            out = jnp.zeros((jl, wide), F32)
+            for zz, b in enumerate(blocks):
+                b = jnp.where(lane < rows, b, 0.0)
+                b = jnp.concatenate([b, jnp.zeros((jl, wide - LANES), F32)], axis=1)
+                out = out + (pltpu.roll(b, zz * rows, 1) if zz else b)
+            return out[:, :kl]
+
+        vec = along(codes)
+        scales = along(
+            [b * -(rew[i] - (total - rew[i]) / (ns - 1)) for i, b in enumerate(gates_z)]
+        )
         slots = NSUB * jl * cap_line
         ids = lax.broadcasted_iota(jnp.int32, (slots, kl), 0).astype(F32) + 1.0
         one = jnp.zeros((slots, kl), F32)
@@ -312,59 +346,51 @@
         for j in range(jl):
             same = ids == vec[j : j + 1]
             one = jnp.where(same, 1.0, one)
-            scale = jnp.where(same, vec[jl + j : jl + j + 1], scale)
+            scale = jnp.where(same, scales[j : j + 1], scale)
         one = one.astype(BF16)
         sel[g] = one
         scol[g] = jnp.sum(scale, axis=1, keepdims=True)
         sel_t[g] = dot_nt(eye(kl), one).astype(BF16)
 
     def select(k, scaled):
-        def body(g, _):
+        for g in range(8):
             rowsv = buf[k, g // 4, g % 4].reshape(kl, cw)
             out = dot_nn(sel[g], rowsv)
             if scaled:
                 out = out * scol[g]
-            at = pl.ds(pl.multiple_of(g * cap_line, cap_line), cap_line)
             for s in range(NSUB):
                 for j in range(jl):
                     r = (s * jl + j) * cap_line
-                    xq[j, at, s * cw : (s + 1) * cw] = out[r : r + cap_line]
-            return 0
-
-        lax.fori_loop(0, 8, body, 0)
+                    xq[j, g * cap_line : (g + 1) * cap_line, s * cw : (s + 1) * cw] = out[
+                        r : r + cap_line
+                    ]
         xs[k] = xq[...].astype(BF16)
 
     def accumulate(i, slot, k):
         half = h // 2
-
-        def body(t, _):
-            j = t // 2
-            r = pl.ds(pl.multiple_of((t % 2) * half, half), half)
-            acc[i, j, r] += dot_nt(wslot[slot, j, r], xs[k, j])
-            return 0
-
-        lax.fori_loop(0, 2 * jl, body, 0)
+        for j in range(jl):
+            for r in (slice(0, half), slice(half, h)):
+                acc[i, j, r] += dot_nt(wslot[slot, j, r], xs[k, j])
 
     def wait_w(slot):
         load(wg, 0, slot).wait()
 
     def step(i):
+        @pl.when(i < nk - LOOK)
+        def _():
+            z_start(i + LOOK)
+
         @pl.when(i < nk)
         def _():
             stage_a(i)
 
-        @pl.when((i >= 1) & (i < nk + 1))
-        def _():
-            stage_b(i - 1)
-
-        @pl.when((i >= 2) & (i < nk + 2))
-        def _():
-            stage_c(i - 2)
-
-        @pl.when(i >= 3)
-        def _():
-            stage_d(i - 3)
-
+        for fn, lag in zip((stage_b, stage_c, stage_d), AHEAD):
+
+            @pl.when((i >= lag) & (i < nk + lag))
+            def _():
+                fn(i - lag)
+
+    first = AHEAD[-1]
     stage_a(nk)
     step(0)
     stage_b(nk)
@@ -372,10 +398,11 @@
     stage_c(nk)
     step(2)
     stage_d(nk)
+    lax.fori_loop(3, first, lambda i, _: (step(i), 0)[1], 0)
     lax.fori_loop(0, 8, lambda g, _: (build(g), 0)[1], 0)
 
     def token_chunk(q, _):
-        step(q + 3)
+        step(q + first)
         select(q, False)
         s = 2 * (q % 2)
         wait_w(s)
@@ -393,7 +420,7 @@
     lax.fori_loop(0, NQ, token_chunk, 0)
 
     def cot_chunk(q, _):
-        step(q + NQ + 3)
+        step(q + NQ + first)
         select(q + NQ, True)
         s = 4 + q % 2
         wait_w(s)
@@ -458,28 +485,23 @@
             wait_w(s)
             wait_w(s + 1)
 
-        def body(j, _):
+        for j in range(jl):
             xq[j] = dot_nn(gn[0, j], wslot[s, j]) + dot_nn(gn[1, j], wslot[s + 1, j])
-            return 0
-
-        lax.fori_loop(0, jl, body, 0)
 
         @pl.when(i == 0)
         def _():
             load(wg, 0, s).start()
             load(wu, 0, s + 1).start()
 
-        def back(g, _):
-            at = pl.ds(pl.multiple_of(g * cap_line, cap_line), cap_line)
+        for g in range(8):
+            at = slice(g * cap_line, (g + 1) * cap_line)
             pieces = [
                 xq[j, at, sb * cw : (sb + 1) * cw] for sb in range(NSUB) for j in range(jl)
             ]
             v = jnp.concatenate(pieces, axis=0).astype(BF16)
             o = dot_nn(sel_t[g], v).astype(BF16)
             buf[q, g // 4, g % 4] = o.reshape(ns, rows, cw)
-            return 0
-
-        lax.fori_loop(0, 8, back, 0)
+
         send_core(q).start()
 
     def send_core(q):
@@ -523,7 +545,10 @@
         for o in range(1, ns):
             send_z(q, o).wait_recv()
             total = total + r3[q, o].astype(F32)
-        gt[q] = total.astype(BF16)
+        total = total.astype(BF16)
+        for sub in range(NSUB):
+            at = pl.ds(pl.multiple_of(q * cq + sub * cw, cw), cw)
+            gt[:, at] = dot_nn(take(rows, t, sub), total).astype(BF16)
 
     lags = cfg["lags"]
 
@@ -552,17 +577,67 @@
         return 0
 
     lax.fori_loop(0, NQ, finish_sends, 0)
-    for k in [nk] + list(range(nk)):
-        for o in range(1, ns):
-            z_copy(k, o).wait_send()
     for o in outs:
         o.wait()
 
 
-def weight_kernel(ht, gg, gu, xr, gr, o_gate, o_up, o_down):
-    o_gate[0] = dot_nn(gg[0], xr[0, 0]).astype(BF16)
-    o_up[0] = dot_nn(gu[0], xr[0, 0]).astype(BF16)
-    o_down[0] = dot_nn(ht[0], gr[0, 0]).astype(BF16)
+def weight_kernel(
+    ht, gg, gu, xs, back, o_gate, o_up, o_down, o_back, hv, xv, stage, hsem, xsem, osem
+):
+    jl = ht.shape[0]
+    cq = xs.shape[3]
+    o_back[...] = back[...]
+    lefts = (gg, gu, ht)
+    dests = (o_gate, o_up, o_down)
+
+    def left(i, j):
+        return pltpu.make_async_copy(lefts[i].at[j], hv.at[i, j], hsem.at[i, j])
+
+    def right(k):
+        return pltpu.make_async_copy(xs.at[k], xv.at[k], xsem.at[k])
+
+    def put(q, j, i):
+        at = pl.ds(pl.multiple_of(q * cq, cq), cq)
+        slot = q % 2
+        return pltpu.make_async_copy(
+            stage.at[slot, j, i], dests[i].at[j, :, at], osem.at[slot, j, i]
+        )
+
+    left(0, 0).start()
+    right(0).start()
+    left(1, 0).start()
+    left(2, 0).start()
+    right(NQ).start()
+    for i in range(3):
+        left(i, 1).start()
+    for q in range(1, NQ):
+        right(q).start()
+        right(NQ + q).start()
+
+    def step(q, _):
+        for j in range(jl):
+            for i in range(3):
+                if i != 1 and j == 0:
+                    right(q if i == 0 else NQ + q).wait()
+
+                @pl.when(q == 0)
+                def _():
+                    left(i, j).wait()
+
+                @pl.when(q >= 2)
+                def _():
+                    put(q - 2, j, i).wait()
+
+                k = NQ + q if i == 2 else q
+                stage[q % 2, j, i] = dot_nn(hv[i, j], xv[k, j]).astype(BF16)
+                put(q, j, i).start()
+        return 0
+
+    lax.fori_loop(0, NQ, step, 0)
+    for q in (NQ - 2, NQ - 1):
+        for j in range(jl):
+            for i in range(3):
+                put(q, j, i).wait()
 
 
 def fused(tokens, cotangent, routes, gate_weights, lengths, rewards, w_gate, w_up, w_down):
@@ -583,10 +658,6 @@
         ns=ns, rows=rows, cw=cw, m=m, h=h, jl=jl, cap_line=cap_line, lags=(1, 3, 4, 6)
     )
 
-    def fold(a):
-        return a.reshape(t, NQ, NSUB, cw).transpose(1, 2, 0, 3).reshape(NQ, rows, cw)
-
-    meta = pack_meta(routes, gate_weights, lengths, rewards, experts, jl, ns, rows)
     vmem = pl.BlockSpec(memory_space=pltpu.VMEM)
     hbm = pl.BlockSpec(memory_space=pltpu.HBM)
     dma = pltpu.SemaphoreType.DMA
@@ -595,17 +666,17 @@
         functools.partial(fused_kernel, cfg),
         name="gather_experts_scatter",
         out_shape=(
-            jax.ShapeDtypeStruct((NQ,) + block, BF16),
+            jax.ShapeDtypeStruct((t, d), BF16),
             jax.ShapeDtypeStruct((jl, h, m), BF16),
             jax.ShapeDtypeStruct((jl, h, m), BF16),
             jax.ShapeDtypeStruct((jl, h, m), BF16),
             jax.ShapeDtypeStruct((nk, jl, m, cq), BF16),
         ),
-        in_specs=[vmem] * 3 + [hbm] * 3,
+        in_specs=[vmem] * 6 + [hbm] * 3,
         out_specs=(vmem, hbm, hbm, hbm, hbm),
         scratch_shapes=[
             pltpu.VMEM((nk, 2, lines, ns) + block, BF16),
-            pltpu.VMEM((2, lines, ns) + meta.shape, F32),
+            pltpu.VMEM((2, lines, ns, 2, experts, LANES), F32),
             pltpu.VMEM((NQ, lines, ns) + block, BF16),
             pltpu.VMEM((NQ, 2, ns) + block, BF16),
             pltpu.VMEM((NQ, ns) + block, BF16),
@@ -626,26 +697,24 @@
         compiler_params=pltpu.CompilerParams(
             collective_id=0, has_side_effects=True, vmem_limit_bytes=67043328
         ),
-    )(fold(tokens), fold(cotangent), meta, w_gate, w_up, w_down)
-
-    full = pl.BlockSpec((1, h, m), lambda j, q: (j, 0, 0))
-    out = pl.BlockSpec((1, h, cq), lambda j, q: (j, 0, q))
+    )(tokens, cotangent, routes.T, gate_weights.T, lengths, rewards, w_gate, w_up, w_down)
+
     shape = jax.ShapeDtypeStruct(w_gate.shape, BF16)
-    g_gate, g_up, g_down = pl.pallas_call(
+    g_gate, g_up, g_down, g_tok = pl.pallas_call(
         weight_kernel,
         name="weight_grads",
-        grid=(jl, NQ),
-        out_shape=(shape, shape, shape),
-        in_specs=[
-            full, full, full,
-            pl.BlockSpec((1, 1, m, cq), lambda j, q: (q, j, 0, 0)),
-            pl.BlockSpec((1, 1, m, cq), lambda j, q: (NQ + q, j, 0, 0)),
+        out_shape=(shape, shape, shape, jax.ShapeDtypeStruct((t, d), BF16)),
+        in_specs=[hbm] * 4 + [vmem],
+        out_specs=(hbm, hbm, hbm, vmem),
+        scratch_shapes=[
+            pltpu.VMEM((3, jl, h, m), BF16),
+            pltpu.VMEM((nk, jl, m, cq), BF16),
+            pltpu.VMEM((2, jl, 3, h, cq), BF16),
+            dma((3, jl)), dma((nk,)), dma((2, jl, 3)),
         ],
-        out_specs=(out, out, out),
-        compiler_params=pltpu.CompilerParams(vmem_limit_bytes=48 * 1024 * 1024),
-    )(ht, gg, gu, xs, xs)
-    grad_tokens = back.reshape(NQ, NSUB, t, cw).transpose(2, 0, 1, 3).reshape(t, d)
-    return grad_tokens, g_gate, g_up, g_down
+        compiler_params=pltpu.CompilerParams(vmem_limit_bytes=67043328),
+    )(ht, gg, gu, xs, back)
+    return g_tok, g_gate, g_up, g_down
 
 
 def covered(mesh, tokens_shape, w_shape, rewards_shape):

time: 155 us -> 129 us (0.83)
  Pallas kernels: 141 us -> 126 us
  local copies, waits for them, and re-layouts: 10.2 us -> 0 us
  other arithmetic: 1.87 us -> 0 us
    pallas_call x1, Pallas kernels: 120 us -> 105 us  [fused(): pl.pallas_call(functools.partial(fused_kernel, cfg), name='gather_experts...]
    reshape x8 -> x0, local copies, waits for them, and re-layouts: 4.4 us -> none  [the longest x6 3.54 us: fold(): a.reshape(t, NQ, NSUB, cw).transpose(1, 2, 0, 3).reshape(NQ, rows, cw)]
    unnamed x6 -> x0, local copies, waits for them, and re-layouts: 3.67 us -> none
where the time goes in v2:
time: 129 us; the launch traced here: 128 us
  Pallas kernels  126 us (98%)
  between operations  1.93 us (1%)
    pallas_call x1, Pallas kernels, fused(): pl.pallas_call(functools.partial(fused_kernel, cfg), name='gather_experts...  105 us
    pallas_call x1, Pallas kernels, fused(): pl.pallas_call(weight_kernel, name='weight_grads', out_shape=(shape, shap...  21.6 us

profile of v2, /device:TPU:0, one launch (start us, length us, event | category | flops | bytes accessed | tf_op | source)
XLA Modules:
  0.0 128.4 jit_solution(15952294440041074841)
XLA Ops:
  1.9 104.9 %gather_experts_scatter.1 = (bf16[20,4096]{1,0:T(8,128)(2,1)}, bf16[2,1024,192]{2,1,0:T(8,128)(2,1)}, bf16[2,1024,192]{2,1,0:T(8,128)(2,1)}, bf16[2,1024,192]{2,1,0:T(8,128)(2,1)}, bf16[8,2,192,1024]{3,2,1,0:T(8,128)(2,1)}) custom-call(bf16[20,4096]{1,0:T(8,128)(2,1)} %tok.1, bf16[20,4096]{1,0:T(8,128)(2,1)} %cot.1, s32[2,20]{1,0:T(2,128)} %bitcast.2, ...), custom_call_target="tpu_custom_call" | custom-call | tf_op jit(solution)/shard_map/gather_experts_scatter/pallas_call | solution.py:665
  106.8 21.6 %weight_grads.1 = (bf16[2,1024,4096]{2,1,0:T(8,128)(2,1)}, bf16[2,1024,4096]{2,1,0:T(8,128)(2,1)}, bf16[2,1024,4096]{2,1,0:T(8,128)(2,1)}, bf16[20,4096]{1,0:T(8,128)(2,1)}) custom-call(bf16[2,1024,192]{2,1,0:T(8,128)(2,1)} %get-tuple-element.13.ht, bf16[2,1024,192]{2,1,0:T(8,128)(2,1)} %get-tuple-element.14.gg, bf16[2,1024,192]{2,1,0:T(8,128)(2,1)} %get-tuple-element.15.gu, ...), custom_call_target="tpu_custom_call" | custom-call | tf_op jit(solution)/shard_map/weight_grads/pallas_call | solution.py:703

commit v3 on v2

--- a/solution.py
+++ b/solution.py
@@ -455,19 +455,15 @@
 
     lax.fori_loop(0, 4 * jl, finish, 0)
 
-    def turn(t, _):
-        gn[t // jl, t % jl] = dot_nt(eye(m), ht[1 + t // jl, t % jl]).astype(BF16)
-        return 0
-
-    lax.fori_loop(0, 2 * jl, turn, 0)
+    for i in range(2):
+        for j in range(jl):
+            gn[i, j] = dot_nt(eye(m), ht[1 + i, j]).astype(BF16)
     outs = [
         pltpu.make_async_copy(ht.at[0], h_out, osem.at[0]),
         pltpu.make_async_copy(ht.at[1], gg_out, osem.at[1]),
         pltpu.make_async_copy(ht.at[2], gu_out, osem.at[2]),
         pltpu.make_async_copy(xs, x_out, osem.at[3]),
     ]
-    for o in outs:
-        o.start()
 
     def drain_all(k, _):
         drain(k)
@@ -556,6 +552,11 @@
         @pl.when(i < NQ)
         def _():
             parts(i)
+
+        @pl.when(i == NQ - 1)
+        def _():
+            for o in outs:
+                o.start()
 
         for fn, lag in zip((s1, s2, s3, s4), lags):
 

time: 129 us -> 128 us (level)
  no operation moved by 1% of the time
where the time goes in v3:
time: 128 us
  Pallas kernels  126 us (98%)
  between operations  1.93 us (2%)
    pallas_call x1, Pallas kernels, fused(): pl.pallas_call(functools.partial(fused_kernel, cfg), name='gather_experts...  104 us
    pallas_call x1, Pallas kernels, fused(): pl.pallas_call(weight_kernel, name='weight_grads', out_shape=(shape, shap...  21.6 us

profile of v3, /device:TPU:0, one launch (start us, length us, event | category | flops | bytes accessed | tf_op | source)
XLA Modules:
  0.0 127.9 jit_solution(15381648928818267946)
XLA Ops:
  1.9 104.4 %gather_experts_scatter.1 = (bf16[20,4096]{1,0:T(8,128)(2,1)}, bf16[2,1024,192]{2,1,0:T(8,128)(2,1)}, bf16[2,1024,192]{2,1,0:T(8,128)(2,1)}, bf16[2,1024,192]{2,1,0:T(8,128)(2,1)}, bf16[8,2,192,1024]{3,2,1,0:T(8,128)(2,1)}) custom-call(bf16[20,4096]{1,0:T(8,128)(2,1)} %tok.1, bf16[20,4096]{1,0:T(8,128)(2,1)} %cot.1, s32[2,20]{1,0:T(2,128)} %bitcast.2, ...), custom_call_target="tpu_custom_call" | custom-call | tf_op jit(solution)/shard_map/gather_experts_scatter/pallas_call | solution.py:666
  106.3 21.6 %weight_grads.1 = (bf16[2,1024,4096]{2,1,0:T(8,128)(2,1)}, bf16[2,1024,4096]{2,1,0:T(8,128)(2,1)}, bf16[2,1024,4096]{2,1,0:T(8,128)(2,1)}, bf16[20,4096]{1,0:T(8,128)(2,1)}) custom-call(bf16[2,1024,192]{2,1,0:T(8,128)(2,1)} %get-tuple-element.13.ht, bf16[2,1024,192]{2,1,0:T(8,128)(2,1)} %get-tuple-element.14.gg, bf16[2,1024,192]{2,1,0:T(8,128)(2,1)} %get-tuple-element.15.gu, ...), custom_call_target="tpu_custom_call" | custom-call | tf_op jit(solution)/shard_map/weight_grads/pallas_call | solution.py:704
